TPU v7x, 128 devices: a whole 4x4x4 slice. The times are simulated.
128 devices in a mesh: replica: 2 (over core), fsdp: 16 (over y, x), tensor: 4 (over z).
Axes of the slice: x: 4, y: 4, z: 4, core: 2. Of those that a mesh axis runs over, the one named last changes fastest.
Arguments:
- grads: bfloat16 [2, 2, 4096, 14336], P('replica', None, 'fsdp', 'tensor'), may hold values from -6 to 6
- momentum: bfloat16 [2, 4096, 14336], P(None, 'fsdp', 'tensor'), may hold values from -50 to 50, as said below
- basis: bfloat16 [2, 14336, 512], P(None, 'tensor'), may hold values from -0.046875 to 0.046875
Outputs:
- momentum_new: bfloat16 [2, 4096, 14336], P(None, 'fsdp', 'tensor')
- update: bfloat16 [2, 4096, 14336], P(None, 'fsdp', 'tensor')
- basis_new: bfloat16 [2, 14336, 512], P(None, 'tensor')
Inputs may be any that keep to these rules, and one draw needn't show every extreme that they name: `momentum`: entries are finite.
All inputs are finite; a program needn't handle non-finite values.
Results may differ from a plain program's by a relative error of at most 0.028.
Values may be sent and summed in bfloat16 or wider, within the bound.
A program may use at most 128 MiB of HBM per device.

v0:
```python
import functools
import math
import jax
import jax.numpy as jnp
from jax import lax
from jax.sharding import Mesh
from jax.sharding import PartitionSpec as P

FEATURES = 4096
UNITS = 14336
RANK = 512
FSDP = ("fsdp_0", "fsdp_1")
REPLICA_FSDP_TENSOR = ("replica", "fsdp_0", "fsdp_1", "tensor")
REPLICA_FSDP = ("replica", "fsdp_0", "fsdp_1")
momentum_decay = 0.95


def from_everyone(x, axis):
    size = lax.axis_size(axis)
    return lax.all_to_all(jnp.broadcast_to(x[None], (size, *x.shape)), axis, 0, 0, tiled=True)


def of_everyone(x, axis):
    everything = from_everyone(x, axis)
    return jnp.sum(everything.astype(jnp.float32), axis=0)


def in_blocks(x, dim, size):
    before, after = (x.shape[:dim], x.shape[dim + 1 :])
    return jnp.moveaxis(x.reshape(*before, size, -1, *after), dim, 0)


def piece_ends(length, count):
    unit = 8 if length >= 8 * count else 1
    return [length // unit * k // count * unit for k in range(1, count)]


def own_block(pieces, axes, turns):
    dims = [lax.axis_size(a) for a in axes]
    pieces = pieces.reshape(*dims, *pieces.shape[1:])
    pieces = pieces.transpose(*turns, *range(len(axes), pieces.ndim))
    pieces = pieces.reshape(-1, *pieces.shape[len(axes) :])
    for k in turns:
        pieces = lax.psum_scatter(pieces, axes[k], scatter_dimension=0, tiled=True)
    return pieces[0]


def spread_scatter(x, axes, dim):
    pieces = in_blocks(x, dim, lax.axis_size(axes))
    cut = max(range(1, max(2, pieces.ndim - 1)), key=lambda d: pieces.shape[d])
    count, done = (len(axes), [])
    for initial, section in enumerate(
        jnp.split(pieces, piece_ends(pieces.shape[cut], count), axis=cut)
    ):
        if section.size:
            turns = [(initial + k) % count for k in range(count)]
            done.append(own_block(section, axes, turns))
    return jnp.concatenate(done, axis=cut - 1)


def over_axes(x, axes):
    return functools.reduce(lax.psum, axes, x)


def total_of_pieces(x, axis):
    return lax.all_gather(x, axis).astype(jnp.float32).sum(0)


def orthonormal(projected, factor):

    def solve_one(lower_mat, rows_mat):
        return jax.scipy.linalg.solve_triangular(lower_mat, rows_mat.T, lower=True).T

    return jax.vmap(solve_one)(factor, projected).astype(jnp.bfloat16)


def power_step(total_grad, moment, right):
    blended = (moment.astype(jnp.float32) + total_grad).astype(jnp.bfloat16)
    partial_value = jnp.einsum("wmc,wcr->wmr", blended, right, preferred_element_type=jnp.float32)
    projected = of_everyone(partial_value.astype(jnp.bfloat16), "tensor").astype(jnp.float32)
    gram_local = jnp.einsum(
        "wmr,wms->wrs", projected, projected, preferred_element_type=jnp.float32
    )
    gram_matrix = lax.psum(gram_local.astype(jnp.bfloat16), FSDP).astype(jnp.float32)
    factor = jnp.linalg.cholesky(gram_matrix)
    left_basis = orthonormal(projected, factor)
    half = blended.shape[2] // lax.axis_size("replica")
    offset = lax.axis_index("replica") * half
    kept_half = half // lax.axis_size(FSDP)
    columns = lax.dynamic_slice_in_dim(blended, offset, kept_half * lax.axis_size(FSDP), 2)
    back_piece = spread_scatter(
        jnp.einsum("wmc,wmr->cwr", columns, left_basis, preferred_element_type=jnp.float32).astype(
            jnp.bfloat16
        ),
        FSDP,
        0,
    ).astype(jnp.float32)
    squares = over_axes(jnp.sum(back_piece * back_piece, axis=0), REPLICA_FSDP_TENSOR)
    back_b = back_piece.astype(jnp.bfloat16)
    right_rows = lax.all_gather(back_b, REPLICA_FSDP, axis=0, tiled=True)
    inverse = 1.0 / (jnp.sqrt(squares) + 1e-06)
    normed = (right_rows.astype(jnp.float32) * inverse[None, :, :]).astype(jnp.bfloat16)
    feedback = jnp.einsum(
        "wmr,cwr->wmc", left_basis, right_rows, preferred_element_type=jnp.float32
    )
    momentum_new = (blended.astype(jnp.float32) - (1.0 - momentum_decay) * feedback).astype(
        jnp.bfloat16
    )
    scale = math.sqrt(FEATURES * UNITS / RANK)
    update = (
        scale * jnp.einsum("wmr,cwr->wmc", left_basis, normed, preferred_element_type=jnp.float32)
    ).astype(jnp.bfloat16)
    basis_new = jnp.transpose(normed, (1, 0, 2))
    return (momentum_new, update, basis_new)


def summed_grads(grads):
    return total_of_pieces(grads[0].astype(jnp.float32).astype(jnp.bfloat16), "replica").astype(
        jnp.float32
    )


def shards(grads, momentum, basis):
    return power_step(summed_grads(grads), momentum, basis)


def solution(mesh):
    torus = Mesh(
        mesh.devices.reshape(mesh.shape["replica"], 4, 4, mesh.shape["tensor"]),
        ("replica", "fsdp_0", "fsdp_1", "tensor"),
    )
    return jax.shard_map(
        shards,
        mesh=torus,
        in_specs=(
            P("replica", None, FSDP, "tensor"),
            P(None, FSDP, "tensor"),
            P(None, "tensor", None),
        ),
        out_specs=(P(None, FSDP, "tensor"), P(None, FSDP, "tensor"), P(None, "tensor", None)),
        check_vma=False,
    )
```

profile of v0, /device:TPU:1, one launch (start us, length us, event | category | flops | bytes accessed | tf_op | source)
XLA Modules:
  0.0 627.0 jit_solution(4297394936807727248)
XLA Ops:
  7.2 0.7 all-gather.3.cloned.1.call-update
  7.9 26.3 %all-gather.3.cloned.1.call-done = bf16[2,2,256,3584]{3,2,1,0:T(8,128)(2,1)} async-done(((bf16[1,2,256,3584]{3,2,1,0:T(8,128)(2,1)}), bf16[2,2,256,3584]{3,2,1,0:T(8,128)(2,1)}) %all-gather.3.cloned.1.call-update) | async-done | bytes 7340048 | tf_op jit(solution)/shard_map/all_gather | solution.py:66
  34.3 5.3 convert_reduce_fusion
  39.6 1.1 add_convert_fusion
  40.7 6.5 %convolution_convert_fusion.2 = bf16[2,256,512]{2,1,0:T(8,128)(2,1)S(1)} fusion(bf16[2,256,3584]{2,1,0:T(8,128)(2,1)S(1)} %add_convert_fusion, bf16[2,3584,512]{2,1,0:T(8,128)(2,1)} %param.5), kind=kOutput, calls=%fused_computation.16 | convolution fusion | flops 1879310336 | bytes 11534336 | tf_op jit(solution)/shard_map/wmc,wcr->wmr/dot_general | solution.py:79
  47.4 30.0 %all_to_all.5 = bf16[4,2,256,512]{3,2,1,0:T(8,128)(2,1)S(1)} all-to-all(bf16[4,2,256,512]{3,2,1,0:T(8,128)(2,1)S(1)} %broadcast_in_dim.4), channel_id=1, replica_groups=mesh['replica'=2,'fsdp_0'=4,'fsdp_1'=4,'tensor'=4] {'tensor'}, dimensions={0} | all-to-all | bytes 4194304 | tf_op jit(solution)/shard_map/all_to_all | solution.py:20
  77.3 0.3 convert_reduce_fusion.1
  77.7 1.5 fusion.38
  79.1 0.6 reduce-scatter.9.cloned.1.call-start
  79.9 1.3 copy.72
  81.2 83.7 %all-reduce.3.cloned.1.call-done = bf16[2,512,512]{1,2,0:T(8,128)(2,1)} async-done(((bf16[2,512,512]{1,2,0:T(8,128)(2,1)}), bf16[2,512,512]{1,2,0:T(8,128)(2,1)}) %all-reduce.3.cloned.1.call-update) | async-done | bytes 1048592 | tf_op jit(solution)/shard_map/psum | solution.py:84
  164.9 1.6 copy.64
  166.5 0.3 fusion.2
  166.8 1.3 copy-done.3
  168.1 23.5 %custom-call.35 = f32[2,128,128]{2,1,0:T(8,128)S(1)} custom-call(f32[2,128,128]{2,1,0:T(8,128)S(1)} %cholesky.274), custom_call_target="Cholesky" | custom-call | tf_op jit(solution)/shard_map/jit(cholesky)/cholesky | solution.py:85
  191.6 19.7 %custom-call.36 = f32[2,1,128,128]{2,3,1,0:T(8,128)S(1)} custom-call(f32[2,1,128,128]{3,2,1,0:T(8,128)S(1)} %select_bitcast_fusion.2), custom_call_target="InvertDiagBlocksLowerTriangular" | custom-call | tf_op jit(solution)/shard_map/jit(cholesky)/cholesky | solution.py:85
  211.6 1.5 constant_dynamic-update-slice_fusion.3
  213.1 1.5 convolution_subtract_fusion
  214.6 23.5 %custom-call.37 = f32[2,128,128]{2,1,0:T(8,128)S(1)} custom-call(f32[2,128,128]{2,1,0:T(8,128)S(1)} %cholesky.278), custom_call_target="Cholesky" | custom-call | tf_op jit(solution)/shard_map/jit(cholesky)/cholesky | solution.py:85
  238.1 19.8 %custom-call.38 = f32[2,1,128,128]{2,3,1,0:T(8,128)S(1)} custom-call(f32[2,1,128,128]{3,2,1,0:T(8,128)S(1)} %get-tuple-element.30), custom_call_target="InvertDiagBlocksLowerTriangular" | custom-call | tf_op jit(solution)/shard_map/jit(cholesky)/cholesky | solution.py:85
  257.9 0.4 convolution_dynamic-update-slice_fusion
  258.3 1.6 convolution_subtract_fusion.3
  259.9 23.5 %custom-call.39 = f32[2,128,128]{2,1,0:T(8,128)S(1)} custom-call(f32[2,128,128]{2,1,0:T(8,128)S(1)} %cholesky.283), custom_call_target="Cholesky" | custom-call | tf_op jit(solution)/shard_map/jit(cholesky)/cholesky | solution.py:85
  283.4 19.7 %custom-call.40 = f32[2,1,128,128]{2,3,1,0:T(8,128)S(1)} custom-call(f32[2,1,128,128]{3,2,1,0:T(8,128)S(1)} %get-tuple-element.28), custom_call_target="InvertDiagBlocksLowerTriangular" | custom-call | tf_op jit(solution)/shard_map/jit(cholesky)/cholesky | solution.py:85
  303.1 0.3 convolution_dynamic-update-slice_fusion.1
  303.4 1.5 convolution_subtract_fusion.5
  304.9 23.7 %custom-call.41 = f32[2,128,128]{2,1,0:T(8,128)S(1)} custom-call(f32[2,128,128]{2,1,0:T(8,128)S(1)} %convolution_subtract_fusion.5), custom_call_target="Cholesky" | custom-call | tf_op jit(solution)/shard_map/jit(cholesky)/cholesky | solution.py:85
  328.9 1.7 select_select_fusion
  330.7 14.5 %while.1 = (s32[]{:T(128)}, f32[2,512,512]{2,1,0:T(8,128)}, s32[4,2]{0,1:T(2,128)S(1)}, f32[4,2,128,128]{3,2,0,1:T(8,128)}, s32[]{:T(128)}) while((s32[]{:T(128)}, f32[2,512,512]{2,1,0:T(8,128)}, s32[4,2]{0,1:T(2,128)S(1)}, f32[4,2,128,128]{3,2,0,1:T(8,128)}, s32[]{:T(128)}) %tuple.36), condition=%wide.while_cond, body=%wide.while_body.sunk | while | flops 2 | bytes 263277 | solution.py:72
  330.8 0.6 fusion.50
  331.4 3.0 bitcast_dynamic-update-slice_fusion.2
  334.4 0.6 fusion.50
  335.0 3.0 bitcast_dynamic-update-slice_fusion.2
  338.0 0.6 fusion.50
  338.6 3.0 bitcast_dynamic-update-slice_fusion.2
  341.7 0.6 fusion.50
  342.3 2.9 bitcast_dynamic-update-slice_fusion.2
  345.2 79.4 %custom-call.42 = f32[2,4,128,128]{2,3,1,0:T(8,128)S(1)} custom-call(f32[2,4,128,128]{3,2,1,0:T(8,128)} %bitcast.91), custom_call_target="InvertDiagBlocksLowerTriangular" | custom-call | tf_op jit(solution)/shard_map/vmap(jit(_solve_triangular))/triangular_solve | solution.py:72
  424.7 0.4 fusion.37
  425.1 1.3 convolution_subtract_fusion.2
  426.4 0.4 fusion.36
  426.8 1.6 convolution_subtract_fusion.1
  428.4 0.4 fusion.35
  428.8 1.7 convolution_subtract_fusion.4
  430.5 0.4 convolution_convert_fusion.3
  430.9 3.0 fusion.1
  433.9 5.9 copy.77
  439.8 2.4 fusion.34
  442.3 1.5 copy.79
  443.8 1.5 copy.95
  445.3 26.8 %reduce-scatter.9.cloned.1.call-done = bf16[4,56,2,512]{3,1,2,0:T(8,128)(2,1)} async-done(((bf16[16,56,2,512]{3,1,2,0:T(8,128)(2,1)}), bf16[4,56,2,512]{3,1,2,0:T(8,128)(2,1)}) %reduce-scatter.9.cloned.1.call-update) | async-done | bytes 458768 | tf_op jit(solution)/shard_map/reduce_scatter | solution.py:44
  472.2 30.1 %reduce-scatter.5.cloned.1.call-done = bf16[4,56,2,512]{3,1,2,0:T(8,128)(2,1)} async-done(((bf16[16,56,2,512]{3,1,2,0:T(8,128)(2,1)}), bf16[4,56,2,512]{3,1,2,0:T(8,128)(2,1)}) %reduce-scatter.5.cloned.1.call-update) | async-done | bytes 458768 | tf_op jit(solution)/shard_map/reduce_scatter | solution.py:44
  502.4 21.0 %reduce-scatter.11.cloned.1.call-done = bf16[1,56,2,512]{3,1,2,0:T(8,128)(2,1)} async-done(((bf16[4,56,2,512]{3,1,2,0:T(8,128)(2,1)}), bf16[1,56,2,512]{3,1,2,0:T(8,128)(2,1)}) %reduce-scatter.11.cloned.1.call-update) | async-done | bytes 114704 | tf_op jit(solution)/shard_map/reduce_scatter | solution.py:44
  523.4 23.3 %reduce-scatter.7.cloned.1.call-done = bf16[1,56,2,512]{3,1,2,0:T(8,128)(2,1)} async-done(((bf16[4,56,2,512]{3,1,2,0:T(8,128)(2,1)}), bf16[1,56,2,512]{3,1,2,0:T(8,128)(2,1)}) %reduce-scatter.7.cloned.1.call-update) | async-done | bytes 114704 | tf_op jit(solution)/shard_map/reduce_scatter | solution.py:44
  546.8 1.7 pad_maximum_fusion.1
  548.4 1.0 multiply_reduce_fusion
  549.5 5.1 psum.36
  554.6 8.4 %psum.37 = f32[2,512]{1,0:T(2,128)S(1)} all-reduce(f32[2,512]{1,0:T(2,128)S(1)} %psum.36), channel_id=1, replica_groups=mesh['replica'=2,'fsdp_0'=4,'fsdp_1'=4,'tensor'=4] {'fsdp_0'}, use_global_device_ids=true, to_apply=%region_17.18 | all-reduce | flops 1024 | bytes 8192 | tf_op jit(solution)/shard_map/psum | solution.py:62
  563.0 6.5 %psum.38 = f32[2,512]{1,0:T(2,128)S(1)} all-reduce(f32[2,512]{1,0:T(2,128)S(1)} %psum.37), channel_id=1, replica_groups=mesh['replica'=2,'fsdp_0'=4,'fsdp_1'=4,'tensor'=4] {'fsdp_1'}, use_global_device_ids=true, to_apply=%region_18.19 | all-reduce | flops 1024 | bytes 8192 | tf_op jit(solution)/shard_map/psum | solution.py:62
  569.5 9.2 %psum.39 = f32[2,512]{1,0:T(2,128)S(1)} all-reduce(f32[2,512]{1,0:T(2,128)S(1)} %psum.38), channel_id=1, replica_groups=mesh['replica'=2,'fsdp_0'=4,'fsdp_1'=4,'tensor'=4] {'tensor'}, use_global_device_ids=true, to_apply=%region_19.20 | all-reduce | flops 1024 | bytes 8192 | tf_op jit(solution)/shard_map/psum | solution.py:62
  578.8 24.0 %all-gather.5.cloned.1.call-done = bf16[3584,2,512]{2,0,1:T(8,128)(2,1)} async-done(((bf16[112,2,512]{2,0,1:T(8,128)(2,1)}), bf16[3584,2,512]{2,0,1:T(8,128)(2,1)}) %all-gather.5.cloned.1.call-update) | async-done | bytes 7340048 | tf_op jit(solution)/shard_map/all_gather | solution.py:100
  602.8 8.3 %subtract_convert_fusion = bf16[2,256,3584]{2,1,0:T(8,128)(2,1)} fusion(bf16[2,256,3584]{2,1,0:T(8,128)(2,1)} %copy-done, bf16[3584,2,512]{2,0,1:T(8,128)(2,1)} %all-gather.5.cloned.1.call-done, bf16[2,128,256]{2,1,0:T(8,128)(2,1)S(1)} %convolution_convert_fusion.3, bf16[2,128,256]{2,1,0:T(8,128)(2,1)S(1)} %get-tuple-element.34, ...), kind=kOutput, calls=%fused_computation.5 | convolution fusion | flops 1888485376 | bytes 15204352 | tf_op jit(solution)/shard_map/wmr,cwr->wmc/dot_general | solution.py:103
  611.1 4.3 multiply_convert_fusion.1
  615.4 4.5 fusion
  (48 shorter events, 1.7 us)
Async XLA Ops:
  7.2 27.1 %all-gather.3.cloned.1.call-start = ((), (), s32[]{:S(2)}) async-start(), calls=%async_computation.5 | async-start | bytes 11010048 | tf_op jit(solution)/shard_map/all_gather | solution.py:66
  7.9 157.0 %all-reduce.3.cloned.1.call-start = ((), (), s32[]{:S(2)}) async-start(), calls=%async_computation.6 | async-start | bytes 2097152 | tf_op jit(solution)/shard_map/psum | solution.py:84
  34.3 5.3 copy-start.6
  40.7 6.5 %copy-start = (bf16[2,256,3584]{2,1,0:T(8,128)(2,1)}, bf16[2,256,3584]{2,1,0:T(8,128)(2,1)S(1)}, u32[]{:S(2)}) copy-start(bf16[2,256,3584]{2,1,0:T(8,128)(2,1)S(1)} %add_convert_fusion) | copy-start | bytes 11010052
  79.1 393.0 %reduce-scatter.9.cloned.1.call-start = ((), (), s32[]{:S(2)}) async-start(), calls=%async_computation.9 | async-start | bytes 2293760 | tf_op jit(solution)/shard_map/reduce_scatter | solution.py:44
  164.9 1.6 copy-start.4
  166.8 1.3 copy-start.3
  328.9 95.7 %copy-start.5 = (f32[2,256,512]{1,2,0:T(8,128)S(1)}, f32[2,256,512]{1,2,0:T(8,128)}, u32[]{:S(2)}) copy-start(f32[2,256,512]{1,2,0:T(8,128)} %copy.72) | copy-start | bytes 3145732
  426.8 4.1 copy-start.1
  443.7 58.6 %reduce-scatter.5.cloned.1.call-start = ((), (), s32[]{:S(2)}) async-start(), calls=%async_computation.7 | async-start | bytes 2293760 | tf_op jit(solution)/shard_map/reduce_scatter | solution.py:44
  445.3 78.1 %reduce-scatter.11.cloned.1.call-start = ((), (), s32[]{:S(2)}) async-start(), calls=%async_computation.10 | async-start | bytes 573440 | tf_op jit(solution)/shard_map/reduce_scatter | solution.py:44
  472.2 74.6 %reduce-scatter.7.cloned.1.call-start = ((), (), s32[]{:S(2)}) async-start(), calls=%async_computation.8 | async-start | bytes 573440 | tf_op jit(solution)/shard_map/reduce_scatter | solution.py:44
  502.4 100.4 %all-gather.5.cloned.1.call-start = ((), (), s32[]{:S(2)}) async-start(), calls=%async_computation.11 | async-start | bytes 7569408 | tf_op jit(solution)/shard_map/all_gather | solution.py:100
  602.8 8.3 %copy-start.2 = (bf16[3584,2,512]{2,0,1:T(8,128)(2,1)S(1)}, bf16[3584,2,512]{2,0,1:T(8,128)(2,1)}, u32[]{:S(2)}) copy-start(bf16[3584,2,512]{2,0,1:T(8,128)(2,1)} %all-gather.5.cloned.1.call-done) | copy-start | bytes 22020100
Sparse Core Ops, SparseCore 0:
  9.6 24.6 all-gather.2
  79.3 85.5 all-reduce.2
  443.9 28.2 reduce-scatter.8
  475.0 27.3 reduce-scatter.4
  504.6 18.7 reduce-scatter.10
  525.7 21.0 reduce-scatter.6
  549.6 53.1 all-gather.4
where the time goes:
time: 632 us; the launch traced here: 627 us
  other arithmetic  249 us (39%)
  waiting for transfers between devices  236 us (37%)
  blocking collectives  59.2 us (9%)
  matrix products  36.4 us (6%)
  local copies, waits for them, and re-layouts  30.5 us (5%)
  between operations  14.8 us (2%)
    another operation x16, other arithmetic, power_step(): factor = jnp.linalg.cholesky(gram_matrix)  154 us
    reduce_scatter x4, waiting for transfers between devices, own_block(): pieces = lax.psum_scatter(pieces, axes[k], scatter_dimension=0, tiled=True)  101 us
    psum x1, waiting for transfers between devices, power_step(): lax.psum(gram_local.astype(jnp.bfloat16), FSDP).astype(jnp.float32)  83.7 us
    another operation x4, other arithmetic, solve_one(): jax.scipy.linalg.solve_triangular(lower_mat, rows_mat.T, lower=True)  81.2 us
    all_to_all x1, blocking collectives, from_everyone(): lax.all_to_all(jnp.broadcast_to(x[None], (size, *x.shape)), axis, 0, 0, t...  30 us
    psum x4, blocking collectives, over_axes(): return functools.reduce(lax.psum, axes, x)  29.3 us
    all_gather x1, waiting for transfers between devices, total_of_pieces(): return lax.all_gather(x, axis).astype(jnp.float32).sum(0)  26.3 us
    all_gather x1, waiting for transfers between devices, power_step(): right_rows = lax.all_gather(back_b, REPLICA_FSDP, axis=0, tiled=True)  24 us
  transfers between devices with their start and end apart: 7, of which 7 were waited for; matrix products, arithmetic and copies ran while one was open for 1% of the time, Pallas kernels for 0%

commit v1 on v0

--- a/solution.py
+++ b/solution.py
@@ -81,7 +81,9 @@
     gram_local = jnp.einsum(
         "wmr,wms->wrs", projected, projected, preferred_element_type=jnp.float32
     )
-    gram_matrix = lax.psum(gram_local.astype(jnp.bfloat16), FSDP).astype(jnp.float32)
+    gram_matrix = jnp.sum(lax.all_gather(gram_local.astype(jnp.bfloat16), FSDP), axis=0).astype(
+        jnp.float32
+    )
     factor = jnp.linalg.cholesky(gram_matrix)
     left_basis = orthonormal(projected, factor)
     half = blended.shape[2] // lax.axis_size("replica")

time: 632 us -> 666 us (1.054)
  waiting for transfers between devices: 236 us -> 261 us
  other arithmetic: 249 us -> 258 us
    all_gather x0 -> x1, waiting for transfers between devices: none -> 109 us  [power_step(): lax.all_gather(gram_local.astype(jnp.bfloat16), FSDP)]
    psum x1 -> x0, waiting for transfers between devices: 83.7 us -> none  [power_step(): lax.psum(gram_local.astype(jnp.bfloat16), FSDP).astype(jnp.float32)]
    reduce_sum x0 -> x1, other arithmetic: none -> 8.93 us  [power_step(): jnp.sum(lax.all_gather(gram_local.astype(jnp.bfloat16), FSDP), axis=0)]
where the time goes in v1:
time: 666 us; the launch traced here: 660 us
  waiting for transfers between devices  261 us (39%)
  other arithmetic  258 us (39%)
  blocking collectives  59 us (9%)
  matrix products  36.4 us (5%)
  local copies, waits for them, and re-layouts  30 us (5%)
  between operations  14.9 us (2%)
    another operation x16, other arithmetic, power_step(): factor = jnp.linalg.cholesky(gram_matrix)  154 us
    all_gather x1, waiting for transfers between devices, power_step(): lax.all_gather(gram_local.astype(jnp.bfloat16), FSDP)  109 us
    reduce_scatter x4, waiting for transfers between devices, own_block(): pieces = lax.psum_scatter(pieces, axes[k], scatter_dimension=0, tiled=True)  100 us
    another operation x4, other arithmetic, solve_one(): jax.scipy.linalg.solve_triangular(lower_mat, rows_mat.T, lower=True)  81.5 us
    all_to_all x1, blocking collectives, from_everyone(): lax.all_to_all(jnp.broadcast_to(x[None], (size, *x.shape)), axis, 0, 0, t...  30 us
    psum x4, blocking collectives, over_axes(): return functools.reduce(lax.psum, axes, x)  29.1 us
    all_gather x1, waiting for transfers between devices, total_of_pieces(): return lax.all_gather(x, axis).astype(jnp.float32).sum(0)  26.3 us
    all_gather x1, waiting for transfers between devices, power_step(): right_rows = lax.all_gather(back_b, REPLICA_FSDP, axis=0, tiled=True)  24.2 us
  transfers between devices with their start and end apart: 7, of which 7 were waited for; matrix products, arithmetic and copies ran while one was open for 1% of the time, Pallas kernels for 0%

profile of v1, /device:TPU:1, one launch (start us, length us, event | category | flops | bytes accessed | tf_op | source)
XLA Modules:
  0.0 660.3 jit_solution(8638468464340141319)
XLA Ops:
  7.2 0.7 all-gather.5.cloned.1.call-update
  7.9 26.3 %all-gather.5.cloned.1.call-done = bf16[2,2,256,3584]{3,2,1,0:T(8,128)(2,1)} async-done(((bf16[1,2,256,3584]{3,2,1,0:T(8,128)(2,1)}), bf16[2,2,256,3584]{3,2,1,0:T(8,128)(2,1)}) %all-gather.5.cloned.1.call-update) | async-done | bytes 7340048 | tf_op jit(solution)/shard_map/all_gather | solution.py:66
  34.3 5.3 convert_reduce_fusion
  39.6 1.1 add_convert_fusion
  40.7 6.5 convolution_convert_fusion.2
  47.4 30.0 %all_to_all.5 = bf16[4,2,256,512]{3,2,1,0:T(8,128)(2,1)S(1)} all-to-all(bf16[4,2,256,512]{3,2,1,0:T(8,128)(2,1)S(1)} %broadcast_in_dim.4), channel_id=1, replica_groups=mesh['replica'=2,'fsdp_0'=4,'fsdp_1'=4,'tensor'=4] {'tensor'}, dimensions={0} | all-to-all | bytes 4194304 | tf_op jit(solution)/shard_map/all_to_all | solution.py:20
  77.7 1.5 fusion.38
  79.1 0.5 reduce-scatter.9.cloned.1.call-start
  79.8 1.3 copy.70
  81.1 109.0 %all-gather.9.cloned.1.call-done = bf16[32,512,512]{2,1,0:T(8,128)(2,1)} async-done(((bf16[2,512,512]{2,1,0:T(8,128)(2,1)}), bf16[32,512,512]{2,1,0:T(8,128)(2,1)}) %all-gather.9.cloned.1.call-update) | async-done | bytes 16777232 | tf_op jit(solution)/shard_map/all_gather | solution.py:84
  190.2 8.9 %reduce_sum.41 = bf16[2,512,512]{2,1,0:T(8,128)(2,1)S(1)} reduce(bf16[16,2,512,512]{3,2,1,0:T(8,128)(2,1)} %bitcast.81, bf16[]{:T(256)} %constant.172.clone.1), dimensions={0}, to_apply=%region_2.0 | reduce | flops 7864320 | bytes 17825794 | tf_op jit(solution)/shard_map/reduce_sum | solution.py:84
  199.1 0.5 copy.61
  199.6 0.5 copy.62
  200.2 0.3 fusion.2
  200.5 1.3 copy-done.3
  201.9 23.5 %custom-call.35 = f32[2,128,128]{2,1,0:T(8,128)S(1)} custom-call(f32[2,128,128]{2,1,0:T(8,128)S(1)} %cholesky.274), custom_call_target="Cholesky" | custom-call | tf_op jit(solution)/shard_map/jit(cholesky)/cholesky | solution.py:87
  225.6 19.7 %custom-call.36 = f32[2,1,128,128]{2,3,1,0:T(8,128)S(1)} custom-call(f32[2,1,128,128]{3,2,1,0:T(8,128)S(1)} %select_bitcast_fusion.2), custom_call_target="InvertDiagBlocksLowerTriangular" | custom-call | tf_op jit(solution)/shard_map/jit(cholesky)/cholesky | solution.py:87
  245.3 1.5 constant_dynamic-update-slice_fusion.3
  246.8 1.5 convolution_subtract_fusion
  248.3 23.6 %custom-call.37 = f32[2,128,128]{2,1,0:T(8,128)S(1)} custom-call(f32[2,128,128]{2,1,0:T(8,128)S(1)} %cholesky.278), custom_call_target="Cholesky" | custom-call | tf_op jit(solution)/shard_map/jit(cholesky)/cholesky | solution.py:87
  272.0 19.7 %custom-call.38 = f32[2,1,128,128]{2,3,1,0:T(8,128)S(1)} custom-call(f32[2,1,128,128]{3,2,1,0:T(8,128)S(1)} %get-tuple-element.30), custom_call_target="InvertDiagBlocksLowerTriangular" | custom-call | tf_op jit(solution)/shard_map/jit(cholesky)/cholesky | solution.py:87
  291.7 0.4 convolution_dynamic-update-slice_fusion
  292.1 1.6 convolution_subtract_fusion.3
  293.6 23.5 %custom-call.39 = f32[2,128,128]{2,1,0:T(8,128)S(1)} custom-call(f32[2,128,128]{2,1,0:T(8,128)S(1)} %cholesky.283), custom_call_target="Cholesky" | custom-call | tf_op jit(solution)/shard_map/jit(cholesky)/cholesky | solution.py:87
  317.1 19.9 %custom-call.40 = f32[2,1,128,128]{2,3,1,0:T(8,128)S(1)} custom-call(f32[2,1,128,128]{3,2,1,0:T(8,128)S(1)} %get-tuple-element.28), custom_call_target="InvertDiagBlocksLowerTriangular" | custom-call | tf_op jit(solution)/shard_map/jit(cholesky)/cholesky | solution.py:87
  337.3 1.5 convolution_subtract_fusion.5
  338.8 23.5 %custom-call.41 = f32[2,128,128]{2,1,0:T(8,128)S(1)} custom-call(f32[2,128,128]{2,1,0:T(8,128)S(1)} %convolution_subtract_fusion.5), custom_call_target="Cholesky" | custom-call | tf_op jit(solution)/shard_map/jit(cholesky)/cholesky | solution.py:87
  362.7 1.7 select_select_fusion
  364.4 14.5 %while.1 = (s32[]{:T(128)}, f32[2,512,512]{2,1,0:T(8,128)}, s32[4,2]{0,1:T(2,128)S(1)}, f32[4,2,128,128]{3,2,0,1:T(8,128)}, s32[]{:T(128)}) while((s32[]{:T(128)}, f32[2,512,512]{2,1,0:T(8,128)}, s32[4,2]{0,1:T(2,128)S(1)}, f32[4,2,128,128]{3,2,0,1:T(8,128)}, s32[]{:T(128)}) %tuple.36), condition=%wide.while_cond, body=%wide.while_body.sunk | while | flops 2 | bytes 263277 | solution.py:72
  364.5 0.6 fusion.50
  365.1 3.0 bitcast_dynamic-update-slice_fusion.2
  368.1 0.6 fusion.50
  368.7 3.0 bitcast_dynamic-update-slice_fusion.2
  371.8 0.6 fusion.50
  372.4 3.0 bitcast_dynamic-update-slice_fusion.2
  375.4 0.6 fusion.50
  376.0 2.9 bitcast_dynamic-update-slice_fusion.2
  379.0 79.7 %custom-call.42 = f32[2,4,128,128]{2,3,1,0:T(8,128)S(1)} custom-call(f32[2,4,128,128]{3,2,1,0:T(8,128)} %bitcast.93), custom_call_target="InvertDiagBlocksLowerTriangular" | custom-call | tf_op jit(solution)/shard_map/vmap(jit(_solve_triangular))/triangular_solve | solution.py:72
  458.6 0.4 fusion.37
  459.1 1.3 convolution_subtract_fusion.2
  460.4 0.4 fusion.36
  460.8 1.6 convolution_subtract_fusion.1
  462.4 0.4 fusion.35
  462.8 1.7 convolution_subtract_fusion.4
  464.5 0.4 convolution_convert_fusion.3
  464.9 3.0 fusion.1
  467.9 5.9 copy.75
  473.8 2.4 fusion.34
  476.3 1.5 copy.77
  477.8 1.5 copy.92
  479.3 25.9 %reduce-scatter.9.cloned.1.call-done = bf16[4,56,2,512]{3,1,2,0:T(8,128)(2,1)} async-done(((bf16[16,56,2,512]{3,1,2,0:T(8,128)(2,1)}), bf16[4,56,2,512]{3,1,2,0:T(8,128)(2,1)}) %reduce-scatter.9.cloned.1.call-update) | async-done | bytes 458768 | tf_op jit(solution)/shard_map/reduce_scatter | solution.py:44
  505.3 30.1 %reduce-scatter.5.cloned.1.call-done = bf16[4,56,2,512]{3,1,2,0:T(8,128)(2,1)} async-done(((bf16[16,56,2,512]{3,1,2,0:T(8,128)(2,1)}), bf16[4,56,2,512]{3,1,2,0:T(8,128)(2,1)}) %reduce-scatter.5.cloned.1.call-update) | async-done | bytes 458768 | tf_op jit(solution)/shard_map/reduce_scatter | solution.py:44
  535.5 21.0 %reduce-scatter.11.cloned.1.call-done = bf16[1,56,2,512]{3,1,2,0:T(8,128)(2,1)} async-done(((bf16[4,56,2,512]{3,1,2,0:T(8,128)(2,1)}), bf16[1,56,2,512]{3,1,2,0:T(8,128)(2,1)}) %reduce-scatter.11.cloned.1.call-update) | async-done | bytes 114704 | tf_op jit(solution)/shard_map/reduce_scatter | solution.py:44
  556.5 23.3 %reduce-scatter.7.cloned.1.call-done = bf16[1,56,2,512]{3,1,2,0:T(8,128)(2,1)} async-done(((bf16[4,56,2,512]{3,1,2,0:T(8,128)(2,1)}), bf16[1,56,2,512]{3,1,2,0:T(8,128)(2,1)}) %reduce-scatter.7.cloned.1.call-update) | async-done | bytes 114704 | tf_op jit(solution)/shard_map/reduce_scatter | solution.py:44
  579.9 1.7 pad_maximum_fusion.1
  581.5 1.0 multiply_reduce_fusion
  582.6 5.1 psum.28
  587.7 8.4 %psum.29 = f32[2,512]{1,0:T(2,128)S(1)} all-reduce(f32[2,512]{1,0:T(2,128)S(1)} %psum.28), channel_id=1, replica_groups=mesh['replica'=2,'fsdp_0'=4,'fsdp_1'=4,'tensor'=4] {'fsdp_0'}, use_global_device_ids=true, to_apply=%region_17.18 | all-reduce | flops 1024 | bytes 8192 | tf_op jit(solution)/shard_map/psum | solution.py:62
  596.1 6.4 psum.30
  602.6 9.1 %psum.31 = f32[2,512]{1,0:T(2,128)S(1)} all-reduce(f32[2,512]{1,0:T(2,128)S(1)} %psum.30), channel_id=1, replica_groups=mesh['replica'=2,'fsdp_0'=4,'fsdp_1'=4,'tensor'=4] {'tensor'}, use_global_device_ids=true, to_apply=%region_19.20 | all-reduce | flops 1024 | bytes 8192 | tf_op jit(solution)/shard_map/psum | solution.py:62
  611.7 24.2 %all-gather.7.cloned.1.call-done = bf16[3584,2,512]{2,0,1:T(8,128)(2,1)} async-done(((bf16[112,2,512]{2,0,1:T(8,128)(2,1)}), bf16[3584,2,512]{2,0,1:T(8,128)(2,1)}) %all-gather.7.cloned.1.call-update) | async-done | bytes 7340048 | tf_op jit(solution)/shard_map/all_gather | solution.py:102
  635.9 8.3 %subtract_convert_fusion = bf16[2,256,3584]{2,1,0:T(8,128)(2,1)} fusion(bf16[2,256,3584]{2,1,0:T(8,128)(2,1)} %copy-done, bf16[3584,2,512]{2,0,1:T(8,128)(2,1)} %all-gather.7.cloned.1.call-done, bf16[2,128,256]{2,1,0:T(8,128)(2,1)S(1)} %convolution_convert_fusion.3, bf16[2,128,256]{2,1,0:T(8,128)(2,1)S(1)} %get-tuple-element.34, ...), kind=kOutput, calls=%fused_computation.5 | convolution fusion | flops 1888485376 | bytes 15204352 | tf_op jit(solution)/shard_map/wmr,cwr->wmc/dot_general | solution.py:105
  644.2 4.3 multiply_convert_fusion.1
  648.5 4.5 fusion
  (48 shorter events, 2.3 us)
Async XLA Ops:
  7.2 27.1 %all-gather.5.cloned.1.call-start = ((), (), s32[]{:S(2)}) async-start(), calls=%async_computation.5 | async-start | bytes 11010048 | tf_op jit(solution)/shard_map/all_gather | solution.py:66
  7.9 182.3 %all-gather.9.cloned.1.call-start = ((), (), s32[]{:S(2)}) async-start(), calls=%async_computation.11 | async-start | bytes 17825792 | tf_op jit(solution)/shard_map/all_gather | solution.py:84
  34.3 5.3 copy-start.5
  40.7 6.5 copy-start
  79.1 426.1 %reduce-scatter.9.cloned.1.call-start = ((), (), s32[]{:S(2)}) async-start(), calls=%async_computation.8 | async-start | bytes 2293760 | tf_op jit(solution)/shard_map/reduce_scatter | solution.py:44
  200.5 1.3 copy-start.3
  362.7 96.0 %copy-start.4 = (f32[2,256,512]{1,2,0:T(8,128)S(1)}, f32[2,256,512]{1,2,0:T(8,128)}, u32[]{:S(2)}) copy-start(f32[2,256,512]{1,2,0:T(8,128)} %copy.70) | copy-start | bytes 3145732
  460.8 4.1 copy-start.1
  477.7 57.7 %reduce-scatter.5.cloned.1.call-start = ((), (), s32[]{:S(2)}) async-start(), calls=%async_computation.6 | async-start | bytes 2293760 | tf_op jit(solution)/shard_map/reduce_scatter | solution.py:44
  479.3 77.2 %reduce-scatter.11.cloned.1.call-start = ((), (), s32[]{:S(2)}) async-start(), calls=%async_computation.9 | async-start | bytes 573440 | tf_op jit(solution)/shard_map/reduce_scatter | solution.py:44
  505.3 74.6 %reduce-scatter.7.cloned.1.call-start = ((), (), s32[]{:S(2)}) async-start(), calls=%async_computation.7 | async-start | bytes 573440 | tf_op jit(solution)/shard_map/reduce_scatter | solution.py:44
  535.4 100.4 %all-gather.7.cloned.1.call-start = ((), (), s32[]{:S(2)}) async-start(), calls=%async_computation.10 | async-start | bytes 7569408 | tf_op jit(solution)/shard_map/all_gather | solution.py:102
  635.9 8.3 %copy-start.2 = (bf16[3584,2,512]{2,0,1:T(8,128)(2,1)S(1)}, bf16[3584,2,512]{2,0,1:T(8,128)(2,1)}, u32[]{:S(2)}) copy-start(bf16[3584,2,512]{2,0,1:T(8,128)(2,1)} %all-gather.7.cloned.1.call-done) | copy-start | bytes 22020100
Sparse Core Ops, SparseCore 0:
  9.6 24.6 all-gather.4
  79.3 110.8 all-gather.8
  477.9 27.3 reduce-scatter.8
  508.1 27.2 reduce-scatter.4
  537.7 18.8 reduce-scatter.10
  558.8 21.0 reduce-scatter.6
  582.7 53.1 all-gather.6
